TPU v7x, 32 devices: a 4x4x1 block of a 4x4x8 slice. The times are simulated.
32 devices in a mesh: dp: 1 (over z), c: 4 (over y), r: 8 (over x, core).
Axes of the slice: x: 4, y: 4, z: 1, core: 2. Of those that a mesh axis runs over, the one named last changes fastest.
The devices are a block of a 4x4x8 slice.
Arguments:
- x: bfloat16 [6144, 3584], P(('dp', 'r'), 'c')
- w: bfloat16 [3584, 28672], P('r', 'c')
- dy: bfloat16 [6144, 28672], P(('dp', 'r'), 'c')
Outputs:
- output 1: bfloat16 [6144, 3584], P(('dp', 'r'), 'c')
- output 2: float32 [3584, 28672], P(('dp', 'r'), 'c')
All inputs are finite; a program needn't handle non-finite values.
Results may differ from a plain program's by a relative error of at most 0.001.
Values are sent between devices in bfloat16 or wider.
A program may use at most 768 MiB of HBM per device.

v0:
```python
import jax
import jax.numpy as jnp
from jax import lax
from jax.sharding import PartitionSpec as P


def solution(mesh):
    def local(x, w, dy):
        w_col = lax.all_gather(w, "r", axis=0, tiled=True)
        dx_part = lax.dot_general(dy, w_col, (((1,), (1,)), ((), ())),
                                  preferred_element_type=jnp.float32)
        dx = lax.psum_scatter(dx_part, "c", scatter_dimension=1, tiled=True).astype(jnp.bfloat16)
        x_row = lax.all_gather(x, "c", axis=1, tiled=True)
        dw_part = lax.dot_general(x_row, dy, (((0,), (0,)), ((), ())),
                                  preferred_element_type=jnp.float32)
        dw = lax.psum_scatter(dw_part, "r", scatter_dimension=0, tiled=True)
        return dx, dw

    act = P(("dp", "r"), "c")
    return jax.shard_map(local, mesh=mesh, in_specs=(act, P("r", "c"), act),
                         out_specs=(act, act), check_vma=False)
```

profile of v0, /device:TPU:101, one launch (start us, length us, event | category | flops | bytes accessed | tf_op | source)
XLA Modules:
  0.0 903.0 jit_solution(13685482074217180661)
XLA Ops:
  7.2 0.1 all-gather.3.cloned.1.call-start
  7.2 0.7 all-gather.3.cloned.1.call-update
  8.0 0.1 all-gather.5.cloned.1.call-start
  8.0 0.7 all-gather.5.cloned.1.call-update
  8.8 0.1 reduce-scatter.5.cloned.1.call-start
  8.8 232.2 %all-gather.3.cloned.1.call-done = bf16[3584,7168]{1,0:T(8,128)(2,1)} async-done(((bf16[448,7168]{1,0:T(8,128)(2,1)}), bf16[3584,7168]{1,0:T(8,128)(2,1)}) %all-gather.3.cloned.1.call-update) | async-done | bytes 51380240 | tf_op jit(solution)/shard_map/all_gather | solution.py:9
  241.1 48.5 %fusion = f32[768,3584]{1,0:T(8,128)} fusion(bf16[768,7168]{1,0:T(8,128)(2,1)} %param.5, bf16[3584,7168]{1,0:T(8,128)(2,1)} %all-gather.3.cloned.1.call-done), kind=kOutput, calls=%fused_computation | convolution fusion | flops 39460012032 | bytes 73400320 | tf_op jit(solution)/shard_map/dot_general | solution.py:10
  289.6 0.1 reduce-scatter.5.cloned.1.call-update
  289.7 0.1 reduce-scatter.7.cloned.1.call-start
  289.7 10.1 %all-gather.5.cloned.1.call-done = bf16[768,3584]{1,0:T(8,128)(2,1)} async-done(((bf16[768,896]{1,0:T(8,128)(2,1)}), bf16[768,3584]{1,0:T(8,128)(2,1)}) %all-gather.5.cloned.1.call-update) | async-done | bytes 5505040 | tf_op jit(solution)/shard_map/all_gather | solution.py:13
  299.8 49.9 %fusion.1 = f32[3584,7168]{1,0:T(8,128)} fusion(bf16[768,3584]{1,0:T(8,128)(2,1)} %all-gather.5.cloned.1.call-done, bf16[768,7168]{1,0:T(8,128)(2,1)} %param.5), kind=kOutput, calls=%fused_computation.1 | convolution fusion | flops 39460012032 | bytes 119275520 | tf_op jit(solution)/shard_map/dot_general | solution.py:14
  349.8 0.1 reduce-scatter.7.cloned.1.call-update
  349.8 52.2 %reduce-scatter.5.cloned.1.call-done = f32[768,896]{1,0:T(8,128)} async-done(((f32[768,3584]{1,0:T(8,128)}), f32[768,896]{1,0:T(8,128)}) %reduce-scatter.5.cloned.1.call-update) | async-done | bytes 2752528 | tf_op jit(solution)/shard_map/reduce_scatter | solution.py:12
  402.1 3.0 convert_element_type.3
  405.1 491.4 %reduce-scatter.7.cloned.1.call-done = f32[448,7168]{1,0:T(8,128)} async-done(((f32[3584,7168]{1,0:T(8,128)}), f32[448,7168]{1,0:T(8,128)}) %reduce-scatter.7.cloned.1.call-update) | async-done | bytes 12845072
Async XLA Ops:
  7.2 233.9 %all-gather.3.cloned.1.call-start = ((), (), s32[]{:S(2)}) async-start(), calls=%async_computation.2 | async-start | bytes 57802752 | tf_op jit(solution)/shard_map/all_gather | solution.py:9
  8.0 291.9 %all-gather.5.cloned.1.call-start = ((), (), s32[]{:S(2)}) async-start(), calls=%async_computation.4 | async-start | bytes 6881280 | tf_op jit(solution)/shard_map/all_gather | solution.py:13
  8.8 393.3 %reduce-scatter.5.cloned.1.call-start = ((), (), s32[]{:S(2)}) async-start(), calls=%async_computation.3 | async-start | bytes 13762560 | tf_op jit(solution)/shard_map/reduce_scatter | solution.py:12
  289.7 606.7 %reduce-scatter.7.cloned.1.call-start = ((), (), s32[]{:S(2)}) async-start(), calls=%async_computation.5 | async-start | bytes 115605504
Sparse Core Ops, SparseCore 0:
  9.6 231.3 all-gather.2
  242.6 57.1 all-gather.4
  302.2 99.8 reduce-scatter.4
  404.9 491.4 reduce-scatter.6
where the time goes:
time: 905 us; the launch traced here: 903 us
  waiting for transfers between devices  787 us (87%)
  matrix products  98.5 us (11%)
  between operations  13.8 us (2%)
    unnamed x5, waiting for transfers between devices  493 us
    all_gather x1, waiting for transfers between devices, local(): w_col = lax.all_gather(w, 'r', axis=0, tiled=True)  232 us
    reduce_scatter x1, waiting for transfers between devices, local(): lax.psum_scatter(dx_part, 'c', scatter_dimension=1, tiled=True)  52.2 us
    dot_general x1, matrix products, local(): lax.dot_general(x_row, dy, (((0,), (0,)), ((), ())), preferred_element_ty...  49.9 us
    dot_general x1, matrix products, local(): lax.dot_general(dy, w_col, (((1,), (1,)), ((), ())), preferred_element_ty...  48.5 us
  transfers between devices with their start and end apart: 4, of which 4 were waited for; matrix products, arithmetic and copies ran while one was open for 11% of the time, Pallas kernels for 0%

commit v1 on v0

v1 whole, which is shorter than its diff:
```python
import functools

import jax
import jax.numpy as jnp
from jax import lax
from jax.experimental import pallas as pl
from jax.experimental.pallas import tpu as pltpu
from jax.sharding import PartitionSpec as P

MESH = pl.DeviceIdType.MESH
ROWS = 128
TILE = 1024


def _kernel(nr, nc, x, w, dy, dx, dw, dyg,
            dyb, wv, dwv, xin, xts, x0, xt, pb, rb, st, dxb, dxo,
            sr, sl, ss, fr, fl, fs, qr, ql, qs, qor, qol, qso,
            sx0, rx0, sx1, rx1, sx2, rx2, sp, rp, sd, rd, lsem):
    r = lax.axis_index("r")
    j = lax.axis_index("c")
    i, k = r // 2, lax.rem(r, 2)
    tb, kb = x.shape
    kd, nb = w.shape
    kq = kd // nc
    ncomm = tb // ROWS
    half = nb // 2
    big = 2 * ROWS

    def rot(d):
        return lax.rem(r + d + nr, nr)

    right, left, opp = rot(2), rot(-2), rot(nr // 2)
    sib = r + 1 - 2 * k
    sibright, sibleft, sibopp = lax.rem(sib + 2, nr), lax.rem(sib - 2 + nr, nr), lax.rem(sib + nr // 2, nr)

    def remote(src, dst, s, q, **dev):
        return pltpu.make_async_remote_copy(src_ref=src, dst_ref=dst, send_sem=s, recv_sem=q,
                                            device_id=dev, device_id_type=MESH)

    def rows(c, n=ROWS):
        return pl.ds(pl.multiple_of(c * n, n), n)

    load_x = pltpu.make_async_copy(x, xin, lsem.at[0])
    load_w = pltpu.make_async_copy(w, wv, lsem.at[1])
    load_x.start()
    load_w.start()
    bar = pltpu.get_barrier_semaphore()
    for dc in range(nc):
        for dr in range(nr):
            if dc or dr:
                pl.semaphore_signal(bar, inc=1, device_id={"c": lax.rem(j + dc, nc), "r": lax.rem(r + dr, nr)},
                                    device_id_type=MESH)
    pl.semaphore_wait(bar, nc * nr - 1)

    def own_right(c):
        return remote(dy.at[rows(c)], dyg.at[r, rows(c)], sr.at[c], ql.at[c], r=right)

    def own_left(c):
        return remote(dy.at[rows(c)], dyg.at[r, rows(c)], sl.at[c], qr.at[c], r=left)

    def to_sib(blk, kind, c):
        src = dy.at[rows(c)] if kind == 0 else dyg.at[blk, rows(c)]
        return remote(src, dyg.at[blk, rows(c)], ss.at[kind, c], qs.at[kind, c], r=sib)

    def fwd_right(c):
        return remote(dyg.at[left, rows(c), pl.ds(0, half)], dyg.at[left, rows(c), pl.ds(0, half)],
                      fr.at[c], qol.at[c], r=right)

    def fwd_left(c):
        return remote(dyg.at[right, rows(c), pl.ds(half, half)], dyg.at[right, rows(c), pl.ds(half, half)],
                      fl.at[c], qor.at[c], r=left)

    def opp_sib(h, c):
        return remote(dyg.at[opp, rows(c), pl.ds(h * half, half)], dyg.at[opp, rows(c), pl.ds(h * half, half)],
                      fs.at[h, c], qso.at[h, c], r=sib)

    own_right(0).start()
    own_left(0).start()

    load_x.wait()
    xts[...] = xin[...].T
    for kk in range(2):
        x0[j, kk] = xts[pl.ds(pl.multiple_of(kk * kd + j * kq, 16), kq)]

    def x_spread(dq, kk):
        q = lax.rem(j + dq, nc)
        return remote(xts.at[pl.ds(pl.multiple_of(kk * kd + q * kq, 16), kq)], x0.at[j, kk],
                      sx0.at[dq - 1, kk], rx0.at[dq - 1, kk], c=q)

    def x_cross(d):
        t = lax.rem(r + d, nr)
        return remote(x0.at[t // 2, lax.rem(t, 2)], xt.at[r, pl.ds(pl.multiple_of(j * kq, 16), kq)],
                      sx1.at[d - 1], rx1.at[d - 1], r=t)

    def x_gather(dq):
        mine = xt.at[:, pl.ds(pl.multiple_of(j * kq, 16), kq)]
        return remote(mine, mine, sx2.at[dq - 1], rx2.at[dq - 1], c=lax.rem(j + dq, nc))

    for dq in range(1, nc):
        for kk in range(2):
            x_spread(dq, kk).start()

    def zero(t, _):
        dwv[:, pl.ds(pl.multiple_of(t * TILE, TILE), TILE)] = jnp.zeros((kd, TILE), jnp.float32)
        return 0

    lax.fori_loop(0, nb // TILE, zero, 0)
    for dq in range(1, nc):
        for kk in range(2):
            x_spread(dq, kk).wait_recv()
    for d in range(1, nr):
        x_cross(d).start()
    xt[r, pl.ds(pl.multiple_of(j * kq, 16), kq)] = x0[i, k]
    for c in range(ncomm):
        if c:
            own_right(c).start()
            own_left(c).start()
        to_sib(r, 0, c).start()
    for d in range(1, nr):
        x_cross(d).wait_recv()
    for dq in range(1, nc):
        x_gather(dq).start()
    load_w.wait()
    for dq in range(1, nc):
        x_gather(dq).wait_recv()

    def exchange(s, base, n, ps, dq):
        q = lax.rem(j + dq, nc)
        return remote(pb.at[ps, pl.ds(pl.multiple_of(q * n, n), n)], rb.at[dq - 1, pl.ds(pl.multiple_of(base, n), n)],
                      sp.at[dq - 1, ps], rp.at[dq - 1, s], c=q)

    def owner(blk, off, base, n, own):
        return remote(st.at[pl.ds(pl.multiple_of(base, n), n)],
                      dxb.at[k, pl.ds(pl.multiple_of(off + j * n, n), n)],
                      sd.at[own], rd.at[k, j], c=i, r=blk)

    def reduce(s, blk, off, base, n, ps):
        for dq in range(1, nc):
            exchange(s, base, n, ps, dq).wait_recv()
        total = pb[ps, pl.ds(pl.multiple_of(j * n, n), n)]
        at = pl.ds(pl.multiple_of(base, n), n)
        for dq in range(1, nc):
            total += rb[dq - 1, at]
        st[at] = total.astype(jnp.bfloat16)

    def deliver(blk, off, base, n):
        @pl.when(blk != r)
        def _():
            owner(blk, off, base, n, 1).start()

        @pl.when((blk == r) & (i != j))
        def _():
            owner(blk, off, base, n, 0).start()

        @pl.when((blk == r) & (i == j))
        def _():
            dxb[k, pl.ds(pl.multiple_of(off + j * n, n), n)] = st[pl.ds(pl.multiple_of(base, n), n)]

    def step(s, blk, off, base, n, slot, local, prev, sent):
        m = n * nc
        at = pl.ds(pl.multiple_of(off, m), m)
        buf = dyb.at[slot, pl.ds(0, m)]

        @pl.when(local)
        def _():
            pltpu.make_async_copy(dy.at[at], buf, lsem.at[2]).start()

        @pl.when(jnp.logical_not(local))
        def _():
            pltpu.make_async_copy(dyg.at[blk, at], buf, lsem.at[2]).start()

        @pl.when(sent)
        def _():
            for dq in range(1, nc):
                exchange(s, base, n, slot, dq).wait_send()

        if prev is not None:
            @pl.when(prev[0])
            def _():
                reduce(*prev[1:])
        pltpu.make_async_copy(dy.at[pl.ds(0, m)], buf, lsem.at[2]).wait()

        pb[slot, pl.ds(0, m)] = jnp.zeros((m, kd), jnp.float32)

        def dx_tile(t, _):
            cols = pl.ds(pl.multiple_of(t * TILE, TILE), TILE)
            pb[slot, pl.ds(0, m)] += lax.dot_general(dyb[slot, pl.ds(0, m), cols], wv[:, cols], (((1,), (1,)), ((), ())),
                                                     preferred_element_type=jnp.float32)
            return 0

        lax.fori_loop(0, nb // TILE, dx_tile, 0)
        if prev is not None:
            @pl.when(prev[0])
            def _():
                deliver(*prev[2:6])

        def dw_tile(t, _):
            cols = pl.ds(pl.multiple_of(t * TILE, TILE), TILE)
            dwv[:, cols] += jnp.dot(xt[blk, :, at], dyb[slot, pl.ds(0, m), cols], preferred_element_type=jnp.float32)
            return 0

        lax.fori_loop(0, 1, dw_tile, 0)
        for dq in range(1, nc):
            exchange(s, base, n, slot, dq).start()
        lax.fori_loop(1, nb // TILE, dw_tile, 0)

    n1, n2 = big // nc, ROWS // nc
    nbig = tb // big
    steps1 = 6 * nbig
    steps2 = 2 * ncomm

    def where1(s):
        t = s - 2 * nbig
        kind = lax.rem(t, 4)
        blk = jnp.where(s < nbig, r, jnp.where(s < 2 * nbig, sib, jnp.where(
            kind == 0, left, jnp.where(kind == 1, right, jnp.where(kind == 2, sibleft, sibright)))))
        c = jnp.where(s < 2 * nbig, lax.rem(s, nbig), t // 4)
        return blk, c

    def body1(s, _):
        t = s - 2 * nbig
        kind = lax.rem(t, 4)
        blk, c = where1(s)

        @pl.when((s >= nbig) & (s < 2 * nbig))
        def _():
            for h in range(2):
                to_sib(sib, 0, 2 * c + h).wait_recv()

        @pl.when((s >= 2 * nbig) & (kind == 0))
        def _():
            for h in range(2):
                own_right(2 * c + h).wait_recv()
                fwd_right(2 * c + h).start()
                to_sib(left, 1, 2 * c + h).start()

        @pl.when((s >= 2 * nbig) & (kind == 1))
        def _():
            for h in range(2):
                own_left(2 * c + h).wait_recv()
                fwd_left(2 * c + h).start()
                to_sib(right, 2, 2 * c + h).start()

        @pl.when((s >= 2 * nbig) & (kind == 2))
        def _():
            for h in range(2):
                to_sib(sibleft, 1, 2 * c + h).wait_recv()

        @pl.when((s >= 2 * nbig) & (kind == 3))
        def _():
            for h in range(2):
                to_sib(sibright, 2, 2 * c + h).wait_recv()

        pblk, pc = where1(s - 1)
        step(s, blk, c * big, s * n1, n1, lax.rem(s, 2), s < nbig,
             (s > 0, s - 1, pblk, pc * big, (s - 1) * n1, n1, lax.rem(s + 1, 2)), s >= 2)
        return 0

    lax.fori_loop(0, steps1, body1, 0)
    last = steps1 - 1
    blk, c = where1(last)
    reduce(last, blk, c * big, last * n1, n1, last % 2)
    for ps in range(2):
        for dq in range(1, nc):
            exchange(0, 0, n1, ps, dq).wait_send()
    base2 = steps1 * n1

    def where2(t):
        return jnp.where(lax.rem(t, 2) == 0, opp, sibopp), t // 2

    def body2(t, _):
        blk, c = where2(t)

        @pl.when(lax.rem(t, 2) == 0)
        def _():
            fwd_right(c).wait_recv()
            opp_sib(0, c).start()
            fwd_left(c).wait_recv()
            opp_sib(1, c).start()

        @pl.when(lax.rem(t, 2) == 1)
        def _():
            for h in range(2):
                opp_sib(h, c).wait_recv()

        @pl.when(t == 0)
        def _():
            pblk, pc = where1(last)
            deliver(pblk, pc * big, last * n1, n1)

        pblk, pc = where2(t - 1)
        step(steps1 + t, blk, c * ROWS, base2 + t * n2, n2, lax.rem(t, 2), t < 0,
             (t > 0, steps1 + t - 1, pblk, pc * ROWS, base2 + (t - 1) * n2, n2, lax.rem(t + 1, 2)), t >= 2)
        return 0

    lax.fori_loop(0, steps2, body2, 0)
    end = steps2 - 1
    blk, c = where2(end)

    def flush(t):
        cols = pl.ds(t * TILE, TILE)
        return pltpu.make_async_copy(dwv.at[:, cols], dw.at[:, cols], lsem.at[3 + t])

    for t in range(nb // TILE):
        flush(t).start()
    reduce(steps1 + end, blk, c * ROWS, base2 + end * n2, n2, end % 2)
    deliver(blk, c * ROWS, base2 + end * n2, n2)

    piece = tb // nc
    for kk in range(2):
        for q in range(nc):
            @pl.when(jnp.logical_not((i == j) & (k == kk) & (j == q)))
            def _():
                remote(st.at[pl.ds(0, piece)], dxb.at[kk, pl.ds(0, piece)], sd.at[0], rd.at[kk, q], c=i, r=sib).wait_recv()
    dxo[:, :kd] = dxb[0]
    dxo[:, kd:] = dxb[1]
    put = pltpu.make_async_copy(dxo, dx, lsem.at[0])
    put.start()

    for ps in range(2):
        for dq in range(1, nc):
            exchange(0, 0, n2, ps, dq).wait_send()

    @pl.when(i != j)
    def _():
        remote(st.at[pl.ds(0, piece)], dxb.at[0, pl.ds(0, piece)], sd.at[0], rd.at[0, 0], c=i, r=sib).wait_send()

    others = (nr - 1) * piece
    remote(st.at[pl.ds(0, others)], st.at[pl.ds(0, others)], sd.at[1], rd.at[0, 0], c=i, r=sib).wait_send()
    for c in range(ncomm):
        own_right(c).wait_send()
        own_left(c).wait_send()
        fwd_right(c).wait_send()
        fwd_left(c).wait_send()
        for kind in range(3):
            to_sib(r, kind, c).wait_send()
        for h in range(2):
            opp_sib(h, c).wait_send()
    for dq in range(1, nc):
        for kk in range(2):
            x_spread(dq, kk).wait_send()
        x_gather(dq).wait_send()
    for d in range(1, nr):
        x_cross(d).wait_send()
    for t in range(nb // TILE):
        flush(t).wait()
    put.wait()


def solution(mesh):
    nr, nc = mesh.shape["r"], mesh.shape["c"]

    def local(x, w, dy):
        tb, kb = x.shape
        kd, nb = w.shape
        ncomm = tb // ROWS
        big = 2 * ROWS
        nsteps = 6 * (tb // big) + 2 * ncomm
        bf16, f32 = jnp.bfloat16, jnp.float32
        dma = pltpu.SemaphoreType.DMA
        any_ = pl.BlockSpec(memory_space=pl.ANY)
        out = pl.pallas_call(
            functools.partial(_kernel, nr, nc),
            name="linear_backward",
            out_shape=(jax.ShapeDtypeStruct((tb, kb), bf16), jax.ShapeDtypeStruct((kd, nb), f32),
                       jax.ShapeDtypeStruct((nr, tb, nb), bf16)),
            in_specs=[any_] * 3,
            out_specs=(any_,) * 3,
            scratch_shapes=[
                pltpu.VMEM((2, big, nb), bf16), pltpu.VMEM((kd, nb), bf16), pltpu.VMEM((kd, nb), f32),
                pltpu.VMEM((tb, kb), bf16), pltpu.VMEM((kb, tb), bf16), pltpu.VMEM((nc, 2, kd // nc, tb), bf16),
                pltpu.VMEM((nr, kd, tb), bf16), pltpu.VMEM((2, big, kd), f32),
                pltpu.VMEM((nc - 1, nr * tb // nc, kd), f32), pltpu.VMEM((nr * tb // nc, kd), bf16),
                pltpu.VMEM((2, tb, kd), bf16), pltpu.VMEM((tb, kb), bf16),
                dma((ncomm,)), dma((ncomm,)), dma((3, ncomm)), dma((ncomm,)), dma((ncomm,)), dma((2, ncomm)),
                dma((ncomm,)), dma((ncomm,)), dma((3, ncomm)), dma((ncomm,)), dma((ncomm,)), dma((2, ncomm)),
                dma((nc - 1, 2)), dma((nc - 1, 2)), dma((nr - 1,)), dma((nr - 1,)), dma((nc - 1,)), dma((nc - 1,)),
                dma((nc - 1, 2)), dma((nc - 1, nsteps)), dma((2,)), dma((2, nc)), dma((3 + nb // TILE,)),
            ],
            compiler_params=pltpu.CompilerParams(collective_id=0, has_side_effects=True,
                                                 vmem_limit_bytes=67043328),
        )(x, w, dy)
        return out[0], out[1]

    act = P(("dp", "r"), "c")
    return jax.shard_map(local, mesh=mesh, in_specs=(act, P("r", "c"), act),
                         out_specs=(act, act), check_vma=False)
```

time: 905 us -> 467 us (0.52)
  waiting for transfers between devices: 787 us -> 0 us
  Pallas kernels: 0 us -> 450 us
  matrix products: 98.5 us -> 0 us
  local copies, waits for them, and re-layouts: 0 us -> 13.5 us
  between operations: 13.8 us -> 0.64 us
    unnamed x5 -> x0, waiting for transfers between devices: 493 us -> none
    pallas_call x0 -> x1, Pallas kernels: none -> 450 us  [local(): pl.pallas_call(functools.partial(_kernel, nr, nc), name='linear_backward'...]
    all_gather x2 -> x0, waiting for transfers between devices: 242 us -> none  [the longest x1 232 us: local(): w_col = lax.all_gather(w, 'r', axis=0, tiled=True)]
    dot_general x2 -> x0, matrix products: 98.5 us -> none  [the longest x1 49.9 us: local(): lax.dot_general(x_row, dy, (((0,), (0,)), ((), ())), preferred_element_ty...]
    reduce_scatter x1 -> x0, waiting for transfers between devices: 52.2 us -> none  [local(): lax.psum_scatter(dx_part, 'c', scatter_dimension=1, tiled=True)]
    unnamed x0 -> x2, local copies, waits for them, and re-layouts: none -> 13.5 us
  transfers between devices with their start and end apart: 4 -> 0, of which waited for: 4 -> 0; matrix products, arithmetic and copies ran while one was open for 11% -> 0% of each run, Pallas kernels for 0% -> 0%
where the time goes in v1:
time: 467 us; the launch traced here: 464 us
  Pallas kernels  450 us (96%)
  local copies, waits for them, and re-layouts  13.5 us (3%)
    pallas_call x1, Pallas kernels, local(): pl.pallas_call(functools.partial(_kernel, nr, nc), name='linear_backward'...  450 us
    unnamed x2, local copies, waits for them, and re-layouts  13.5 us

profile of v1, /device:TPU:101, one launch (start us, length us, event | category | flops | bytes accessed | tf_op | source)
XLA Modules:
  0.0 464.1 jit_solution(11117737008056752739)
XLA Ops:
  0.6 449.9 %linear_backward.1 = (bf16[768,896]{1,0:T(8,128)(2,1)}, f32[448,7168]{1,0:T(8,128)}, bf16[8,768,7168]{2,1,0:T(8,128)(2,1)}) custom-call(bf16[768,896]{1,0:T(8,128)(2,1)} %x.1, bf16[448,7168]{1,0:T(8,128)(2,1)} %w.1, bf16[768,7168]{1,0:T(8,128)(2,1)} %dy.1), custom_call_target="tpu_custom_call" | custom-call | tf_op jit(solution)/shard_map/linear_backward/pallas_call | solution.py:362
  450.5 2.5 copy.7
  453.1 11.0 %copy.8 = f32[448,7168]{1,0:T(8,128)} copy(f32[448,7168]{1,0:T(8,128)} %get-tuple-element.9) | data formatting | bytes 25690112

commit v2 on v0

v2 whole, which is shorter than its diff:
```python
import functools

import jax
import jax.numpy as jnp
from jax import lax
from jax.experimental import pallas as pl
from jax.experimental.pallas import tpu as pltpu
from jax.sharding import PartitionSpec as P

MESH = pl.DeviceIdType.MESH
ROWS = 128
FIRST = 3
SUB = 64
TILE = 1024
VMEM = 67043328
PUTS = 4


def _main(nr, nc, x, w, dy, dwv, dxb, dxl, dyg,
          dyb, dyl, wv, xin, xts, x0, xt, pb, pt, rb, rt, st, stl,
          s_own, s_fwd, s_sib, s_opp, q_left, q_right, q_sib, q_fwd, q_opp, s_last, q_last, q_slast,
          s_x, q_x, s_part, q_part, s_dx, q_dx, q_dxl, lsem):
    r = lax.axis_index("r")
    j = lax.axis_index("c")
    i, k = r // 2, lax.rem(r, 2)
    tb = x.shape[0]
    kd, nb = w.shape
    kq = kd // nc
    half = nb // 2
    m = 2 * ROWS
    nbig = tb // m
    early = 6 * nbig
    runs = tb // ROWS - 1
    steps = early + runs
    subs = ROWS // SUB

    def rot(d):
        return lax.rem(r + d + nr, nr)

    right, left, opp = rot(2), rot(-2), rot(nr // 2)
    sib = r + 1 - 2 * k
    sibright, sibleft, sibopp = lax.rem(sib + 2, nr), lax.rem(sib - 2 + nr, nr), lax.rem(sib + nr // 2, nr)

    def remote(src, dst, s, q, **dev):
        return pltpu.make_async_remote_copy(src_ref=src, dst_ref=dst, send_sem=s, recv_sem=q,
                                            device_id=dev, device_id_type=MESH)

    def at(start, size):
        return pl.ds(pl.multiple_of(start, size), size)

    load_x = pltpu.make_async_copy(x, xin, lsem.at[0])
    load_w = pltpu.make_async_copy(w, wv, lsem.at[1])
    load_x.start()
    load_w.start()
    bar = pltpu.get_barrier_semaphore()
    for dc in range(nc):
        for dr in range(nr):
            if dc or dr:
                pl.semaphore_signal(bar, inc=1, device_id={"c": lax.rem(j + dc, nc), "r": lax.rem(r + dr, nr)},
                                    device_id_type=MESH)
    pl.semaphore_wait(bar, nc * nr - 1)

    def own_right(row, size):
        rows = pl.ds(row, size)
        return remote(dy.at[rows], dyg.at[r, rows], s_own.at[0], q_left.at[row // m], r=right)

    def own_left(row, size):
        rows = pl.ds(row, size)
        return remote(dy.at[rows], dyg.at[r, rows], s_own.at[1], q_right.at[row // m], r=left)

    def to_sib(blk, kind, c):
        src = dy.at[at(c * m, m)] if kind == 0 else dyg.at[blk, at(c * m, m)]
        return remote(src, dyg.at[blk, at(c * m, m)], s_sib.at[kind], q_sib.at[kind, c], r=sib)

    def wait_left(c):
        remote(dy.at[at(c * m, m)], dyg.at[left, at(c * m, m)], s_own.at[0], q_left.at[c], r=right).wait_recv()

    def wait_right(c):
        remote(dy.at[at(c * m, m)], dyg.at[right, at(c * m, m)], s_own.at[1], q_right.at[c], r=left).wait_recv()

    def part(blk, h, row, size):
        return dyg.at[blk, at(row, size), pl.ds(h * half, half)]

    def forward(h, row, size, q):
        blk, to = ((left, right), (right, left))[h]
        return remote(part(blk, h, row, size), part(blk, h, row, size), s_fwd.at[h], q_fwd.at[h, q], r=to)

    def opp_in(h, row, size, q):
        return remote(part(opp, h, row, size), part(opp, h, row, size), s_fwd.at[h], q_fwd.at[h, q], r=right)

    def opp_sib(h, row, size, q):
        return remote(part(opp, h, row, size), part(opp, h, row, size), s_opp, q_opp.at[q], r=sib)

    def wait_opp_sib(row, size, q):
        rows = dyg.at[sibopp, at(row, size)]
        remote(rows, rows, s_opp, q_opp.at[q], r=sib).wait_recv()

    def last(h, u, row):
        return dyl.at[pl.ds(pl.multiple_of(row + u * SUB, SUB), SUB), pl.ds(h * half, half)]

    def forward_last(h, u):
        blk, to = ((left, right), (right, left))[h]
        return remote(part(blk, h, tb - ROWS + u * SUB, SUB), last(h, u, 0), s_fwd.at[h], q_last.at[h, u], r=to)

    def sib_last(h, u):
        return remote(last(h, u, 0), last(h, u, ROWS), s_last, q_slast.at[u], r=sib)

    own_right(0, ROWS).start()
    own_left(0, ROWS).start()

    load_x.wait()
    xts[...] = xin[...].T
    for kk in range(2):
        x0[j, kk] = xts[pl.ds(pl.multiple_of(kk * kd + j * kq, 16), kq)]
    mine = pl.ds(pl.multiple_of(j * kq, 16), kq)

    for dq in range(1, nc):
        for kk in range(2):
            q = lax.rem(j + dq, nc)
            remote(xts.at[pl.ds(pl.multiple_of(kk * kd + q * kq, 16), kq)], x0.at[j, kk],
                   s_x.at[0], q_x.at[0], c=q).start()
    spread = remote(x0.at[pl.ds(0, nc - 1)], x0.at[pl.ds(0, nc - 1)], s_x.at[0], q_x.at[0], c=lax.rem(j + 1, nc))

    def zero(t, _):
        dwv[:, at(t * TILE, TILE)] = jnp.zeros((kd, TILE), jnp.float32)
        return 0

    lax.fori_loop(0, nb // TILE, zero, 0)
    with jax.named_scope("xspread"):
        spread.wait_recv()
    for d in range(1, nr):
        t = lax.rem(r + d, nr)
        remote(x0.at[t // 2, lax.rem(t, 2)], xt.at[r, mine], s_x.at[1], q_x.at[1], r=t).start()
    cross = remote(xt.at[pl.ds(0, nr - 1), mine], xt.at[pl.ds(0, nr - 1), mine], s_x.at[1], q_x.at[1], r=right)
    xt[r, mine] = x0[i, k]
    own_right(ROWS, ROWS).start()
    own_left(ROWS, ROWS).start()
    to_sib(r, 0, 0).start()
    for c in range(1, nbig):
        own_right(c * m, m).start()
        own_left(c * m, m).start()
        to_sib(r, 0, c).start()
    with jax.named_scope("xcross"):
        cross.wait_recv()
    for dq in range(1, nc):
        remote(xt.at[:, mine], xt.at[:, mine], s_x.at[2], q_x.at[2], c=lax.rem(j + dq, nc)).start()
    others = pl.ds(0, (nc - 1) * kq)
    gather = remote(xt.at[:, others], xt.at[:, others], s_x.at[2], q_x.at[2], c=lax.rem(j + 1, nc))
    load_w.wait()

    def where(s):
        t = s - 2 * nbig
        kind = lax.rem(t, 4)
        late = s >= early
        blk = jnp.where(s < nbig, r, jnp.where(s < 2 * nbig, sib, jnp.where(
            kind == 0, left, jnp.where(kind == 1, right, jnp.where(kind == 2, sibleft, sibright)))))
        c = 2 * jnp.where(s < 2 * nbig, lax.rem(s, nbig), t // 4)
        blka = jnp.where(late, opp, blk)
        blkb = jnp.where(late, sibopp, blk)
        ca = jnp.where(late, s - early, c)
        cb = jnp.where(late, s - early, c + 1)
        return blka, ca, blkb, cb

    def fetch(src, blk, row, size, slot, to, h):
        rows = src.at[at(row, size)] if blk is None else src.at[blk, at(row, size)]
        return pltpu.make_async_copy(rows, dyb.at[slot, pl.ds(to, size)], lsem.at[2 + h])

    def arrive(s):
        blka, ca, blkb, cb = where(s)
        slot = lax.rem(s, 2)
        t = s - 2 * nbig
        kind = lax.rem(t, 4)
        c = t // 4
        mid = (s >= 2 * nbig) & (s < early)

        @pl.when((s >= nbig) & (s < 2 * nbig))
        def _():
            to_sib(sib, 0, s - nbig).wait_recv()

        for h in range(2):
            @pl.when(mid & (kind == h))
            def _():
                (wait_left, wait_right)[h](c)

                forward(h, 2 * c * ROWS, ROWS, 2 * c).start()

                @pl.when(c < nbig - 1)
                def _():
                    forward(h, (2 * c + 1) * ROWS, ROWS, 2 * c + 1).start()

                @pl.when(c == nbig - 1)
                def _():
                    for u in range(subs):
                        forward_last(h, u).start()

                to_sib((left, right)[h], 1 + h, c).start()

            @pl.when(mid & (kind == 2 + h))
            def _():
                to_sib((sibleft, sibright)[h], 1 + h, c).wait_recv()

        @pl.when(s < nbig)
        def _():
            fetch(dy, None, ca * ROWS, ROWS, slot, 0, 0).start()
            fetch(dy, None, cb * ROWS, ROWS, slot, ROWS, 1).start()

        @pl.when(s >= nbig)
        def _():
            @pl.when(s >= early)
            def _():
                with jax.named_scope("opp"):
                    for h in range(2):
                        opp_in(h, ca * ROWS, ROWS, ca).wait_recv()
                        opp_sib(h, ca * ROWS, ROWS, ca).start()

            fetch(dyg, blka, ca * ROWS, ROWS, slot, 0, 0).start()

            @pl.when(s >= early)
            def _():
                with jax.named_scope("oppsib"):
                    wait_opp_sib(ca * ROWS, ROWS, ca)

            fetch(dyg, blkb, cb * ROWS, ROWS, slot, ROWS, 1).start()

    def exchange(s):
        ps = lax.rem(s, 3)
        for dq in range(1, nc):
            q = lax.rem(j + dq, nc)
            remote(pb.at[ps, pl.ds(pl.multiple_of(q * kq, 16), kq)], rb.at[dq - 1, s], s_part.at[ps], q_part.at[s], c=q).start()

    def exchanged(s):
        ps = lax.rem(s, 3)
        rows = pl.ds(0, (nc - 1) * kq)
        return remote(pb.at[ps, rows], pb.at[ps, rows], s_part.at[ps], q_part.at[s], c=lax.rem(j + 1, nc))

    def sum_step(s):
        exchanged(s).wait_recv()
        acc = pb[lax.rem(s, 3), mine]
        for dq in range(1, nc):
            acc += rb[dq - 1, s]
        st[s] = acc.astype(jnp.bfloat16)

    def send_dx(s, lanes, blk, row, size):
        src = st.at[s, :, lanes]
        share = pl.ds(pl.multiple_of(k * kd + j * kq, 16), kq)
        dst = dxb.at[share, at(row, size)]

        @pl.when(blk != r)
        def _():
            remote(src, dst, s_dx.at[1], q_dx.at[k], c=i, r=blk).start()

        @pl.when((blk == r) & (i != j))
        def _():
            remote(src, dst, s_dx.at[0], q_dx.at[k], c=i, r=blk).start()

        @pl.when((blk == r) & (i == j))
        def _():
            dxb[share, at(row, size)] = st[s, :, lanes]

    def deliver_early(s):
        blka, ca, _, _ = where(s)
        send_dx(s, pl.ds(0, m), blka, ca * ROWS, m)

    def deliver_late(s):
        blka, ca, blkb, cb = where(s)
        send_dx(s, pl.ds(0, ROWS), blka, ca * ROWS, ROWS)
        send_dx(s, pl.ds(ROWS, ROWS), blkb, cb * ROWS, ROWS)

    def exchange_last(u):
        for dq in range(1, nc):
            q = lax.rem(j + dq, nc)
            remote(pt.at[u, pl.ds(pl.multiple_of(q * kq, 16), kq)], rt.at[dq - 1, u], s_part.at[3 + u], q_part.at[steps + u],
                   c=q).start()

    def exchanged_last(u):
        rows = pl.ds(0, (nc - 1) * kq)
        return remote(pt.at[u, rows], pt.at[u, rows], s_part.at[3 + u], q_part.at[steps + u], c=lax.rem(j + 1, nc))

    def sum_last(u):
        exchanged_last(u).wait_recv()
        acc = pt[u, mine]
        for dq in range(1, nc):
            acc += rt[dq - 1, u]
        stl[u] = acc.astype(jnp.bfloat16)

    def deliver_last(u):
        share = pl.ds(pl.multiple_of(k * kd + j * kq, 16), kq)
        for blk in (opp, sibopp):
            remote(stl.at[u], dxl.at[share, at(u * 2 * SUB, 2 * SUB)], s_dx.at[1], q_dxl.at[k], c=i, r=blk).start()

    arrive(jnp.int32(0))
    with jax.named_scope("xgather"):
        gather.wait_recv()

    def dw_tiles(buf, blka, ca, blkb, cb, lo, hi):
        def dw_tile(t, _):
            cols = at(t * TILE, TILE)
            lhs = jnp.concatenate([xt[blka, :, at(ca * ROWS, ROWS)], xt[blkb, :, at(cb * ROWS, ROWS)]], axis=1)
            dwv[:, cols] += jnp.dot(lhs, buf[:, cols], preferred_element_type=jnp.float32)
            return 0

        lax.fori_loop(lo, hi, dw_tile, 0)

    def step(s, _):
        slot, ps = lax.rem(s, 2), lax.rem(s, 3)
        blka, ca, blkb, cb = where(s)

        @pl.when(s >= 3)
        def _():
            exchanged(s - 3).wait_send()

        with jax.named_scope("reduce"):
            @pl.when((s >= 2) & (s <= early))
            def _():
                sum_step(s - 2)

            @pl.when(s >= early)
            def _():
                sum_step(s - 1)

        with jax.named_scope("loadwait"):
            for h in range(2):
                fetch(dyg, r, 0, ROWS, slot, h * ROWS, h).wait()
        pb[ps] = jnp.zeros((kd, m), jnp.float32)

        def dx_tile(t, _):
            cols = at(t * TILE, TILE)
            pb[ps] += lax.dot_general(wv[:, cols], dyb[slot, :, cols], (((1,), (1,)), ((), ())),
                                      preferred_element_type=jnp.float32)
            return 0

        with jax.named_scope("dx"):
            lax.fori_loop(0, nb // TILE, dx_tile, 0)

        dw_tiles(dyb.at[slot], blka, ca, blkb, cb, 0, 1)
        exchange(s)

        @pl.when((s >= 2) & (s < FIRST + 2))
        def _():
            deliver_early(s - 2)

        per = -(-(early - FIRST) // runs)
        for d in range(per):
            old = FIRST + (s - early) * per + d

            @pl.when((s >= early) & (old < early))
            def _():
                deliver_early(old)

        @pl.when(s > early)
        def _():
            deliver_late(s - 1)

        @pl.when(s < early - 1)
        def _():
            arrive(s + 1)

        with jax.named_scope("dw"):
            dw_tiles(dyb.at[slot], blka, ca, blkb, cb, 1, nb // TILE)

        @pl.when((s >= early - 1) & (s < steps - 1))
        def _():
            arrive(s + 1)

        return 0

    lax.fori_loop(0, steps, step, 0)

    for u in range(subs):
        with jax.named_scope("opp"):
            for h in range(2):
                forward_last(h, u).wait_recv()
                sib_last(h, u).start()
        if u == 0:
            pt[...] = jnp.zeros((subs, kd, 2 * SUB), jnp.float32)
        with jax.named_scope("oppsib"):
            both = dyl.at[pl.ds(0, SUB)]
            remote(both, both, s_last, q_slast.at[u], r=sib).wait_recv()

        def dx_tile(t, _):
            cols = at(t * TILE, TILE)
            rhs = jnp.concatenate([dyl[pl.ds(u * SUB, SUB), cols], dyl[pl.ds(ROWS + u * SUB, SUB), cols]], axis=0)
            pt[u] += lax.dot_general(wv[:, cols], rhs, (((1,), (1,)), ((), ())), preferred_element_type=jnp.float32)
            return 0

        with jax.named_scope("dx"):
            lax.fori_loop(0, nb // TILE, dx_tile, 0)
        if u == subs - 1:
            dw_tiles(dyl, opp, runs, sibopp, runs, 0, 1)
        exchange_last(u)
        if u == 0:
            with jax.named_scope("reduce"):
                sum_step(steps - 1)

    deliver_late(steps - 1)
    with jax.named_scope("dw"):
        dw_tiles(dyl, opp, runs, sibopp, runs, 1, nb // TILE)
    for u in range(subs - 1):
        with jax.named_scope("reduce"):
            sum_last(u)
        deliver_last(u)

    for d in range(2):
        remote(dy, dyg.at[r], s_own.at[d], q_left.at[0], r=right).wait_send()
        remote(dyg.at[r, :, pl.ds(0, half)], dyg.at[r, :, pl.ds(0, half)], s_fwd.at[d], q_left.at[0], r=right).wait_send()
    for kind in range(3):
        remote(dy, dyg.at[r], s_sib.at[kind], q_left.at[0], r=right).wait_send()
    sent = dyg.at[r, pl.ds(0, runs * ROWS)]
    remote(sent, sent, s_opp, q_left.at[0], r=right).wait_send()
    sent = dyl.at[pl.ds(0, ROWS)]
    remote(sent, sent, s_last, q_left.at[0], r=right).wait_send()
    for sent in (spread, cross, gather):
        sent.wait_send()
    for s in range(steps - 3, steps):
        exchanged(s).wait_send()
    with jax.named_scope("reduce"):
        sum_last(subs - 1)
    for u in range(subs):
        exchanged_last(u).wait_send()
    deliver_last(subs - 1)

    facing = lax.rem(i - j + nc, nc) == nc // 2
    with jax.named_scope("dxfinal"):
        for kk in range(2):
            own = (i == j) & (k == kk)

            @pl.when(own)
            def _():
                rest = dxb.at[pl.ds(0, kd - kq)]
                remote(rest, rest, s_dx.at[0], q_dx.at[kk], c=i, r=sib).wait_recv()

            @pl.when(facing)
            def _():
                rest = dxb.at[pl.ds(0, kd), pl.ds(0, runs * ROWS)]
                remote(rest, rest, s_dx.at[0], q_dx.at[kk], c=i, r=sib).wait_recv()
                rest = dxl.at[pl.ds(0, kd)]
                remote(rest, rest, s_dx.at[0], q_dxl.at[kk], c=i, r=sib).wait_recv()

            @pl.when(jnp.logical_not(own | facing))
            def _():
                rest = dxb.at[pl.ds(0, kd)]
                remote(rest, rest, s_dx.at[0], q_dx.at[kk], c=i, r=sib).wait_recv()

    with jax.named_scope("drain"):
        @pl.when(i != j)
        def _():
            away = st.at[pl.ds(0, nbig)]
            remote(away, away, s_dx.at[0], q_dx.at[0], c=i, r=sib).wait_send()

        away = st.at[pl.ds(0, early - nbig + runs + subs * 2 * 2 * SUB // m)]
        remote(away, away, s_dx.at[1], q_dx.at[0], c=i, r=sib).wait_send()


def _store(nc, dwv, dxb, dxl, dx, dw, dxo, sem):
    kd = dwv.shape[0]
    tb = dxb.shape[1]
    puts = []
    for p in range(PUTS):
        rows = pl.ds(p * (kd // PUTS), kd // PUTS)
        puts.append(pltpu.make_async_copy(dwv.at[rows], dw.at[rows], sem.at[p]))
    for put in puts:
        put.start()
    r = lax.axis_index("r")
    i, k = r // 2, lax.rem(r, 2)
    facing = lax.rem(i - lax.axis_index("c") + nc, nc) == nc // 2
    dxo[:tb - ROWS] = dxb[:, :tb - ROWS].T
    for kk in range(2):
        rows = pl.ds(kk * kd, kd)
        runs = [dxl[rows, u * 2 * SUB:(u + 1) * 2 * SUB] for u in range(ROWS // SUB)]
        a = jnp.concatenate([run[:, :SUB] for run in runs], axis=1)
        b = jnp.concatenate([run[:, SUB:] for run in runs], axis=1)
        late = jnp.where(facing, jnp.where(k == kk, a, b), dxb[rows, tb - ROWS:])
        dxo[tb - ROWS:, kk * kd:(kk + 1) * kd] = late.T
    puts.append(pltpu.make_async_copy(dxo, dx, sem.at[PUTS]))
    puts[-1].start()
    for put in puts:
        put.wait()


def solution(mesh):
    nr, nc = mesh.shape["r"], mesh.shape["c"]

    def local(x, w, dy):
        tb, kb = x.shape
        kd, nb = w.shape
        m = 2 * ROWS
        nbig, runs, subs = tb // m, tb // ROWS - 1, ROWS // SUB
        nsteps = 6 * nbig + runs
        kq = kd // nc
        bf16, f32 = jnp.bfloat16, jnp.float32
        dma = pltpu.SemaphoreType.DMA
        any_ = pl.BlockSpec(memory_space=pl.ANY)
        vmem = pl.BlockSpec(memory_space=pltpu.VMEM)
        outs = kd * nb * 4 + kb * (tb + 2 * ROWS) * 2
        dwv, dxb, dxl, _ = pl.pallas_call(
            functools.partial(_main, nr, nc),
            name="linear_backward",
            out_shape=(pltpu.VMEM((kd, nb), f32), pltpu.VMEM((kb, tb), bf16),
                       pltpu.VMEM((kb, 2 * ROWS), bf16), jax.ShapeDtypeStruct((nr, tb, nb), bf16)),
            in_specs=[any_] * 3,
            out_specs=(vmem, vmem, vmem, any_),
            scratch_shapes=[
                pltpu.VMEM((2, m, nb), bf16), pltpu.VMEM((m, nb), bf16), pltpu.VMEM((kd, nb), bf16),
                pltpu.VMEM((tb, kb), bf16), pltpu.VMEM((kb, tb), bf16), pltpu.VMEM((nc, 2, kd // nc, tb), bf16),
                pltpu.VMEM((nr, kd, tb), bf16), pltpu.VMEM((3, kd, m), f32), pltpu.VMEM((subs, kd, 2 * SUB), f32),
                pltpu.VMEM((nc - 1, nsteps, kq, m), f32), pltpu.VMEM((nc - 1, subs, kq, 2 * SUB), f32),
                pltpu.VMEM((nsteps, kq, m), bf16), pltpu.VMEM((subs, kq, 2 * SUB), bf16),
                dma((2,)), dma((2,)), dma((3,)), dma, dma((nbig,)), dma((nbig,)), dma((3, nbig)),
                dma((2, runs)), dma((runs,)), dma, dma((2, subs)), dma((subs,)),
                dma((3,)), dma((3,)), dma((3 + subs,)), dma((nsteps + subs,)), dma((2,)), dma((2,)), dma((2,)), dma((4,)),
            ],
            compiler_params=pltpu.CompilerParams(collective_id=0, has_side_effects=True,
                                                 vmem_limit_bytes=VMEM - outs - 2**21),
        )(x, w, dy)
        return pl.pallas_call(
            functools.partial(_store, nc),
            name="store",
            out_shape=(jax.ShapeDtypeStruct((tb, kb), bf16), jax.ShapeDtypeStruct((kd, nb), f32)),
            in_specs=[vmem] * 3,
            out_specs=(any_, any_),
            scratch_shapes=[pltpu.VMEM((tb, kb), bf16), dma((PUTS + 1,))],
            compiler_params=pltpu.CompilerParams(vmem_limit_bytes=2**22),
        )(dwv, dxb, dxl)

    act = P(("dp", "r"), "c")
    return jax.shard_map(local, mesh=mesh, in_specs=(act, P("r", "c"), act),
                         out_specs=(act, act), check_vma=False)
```

time: 905 us -> 408 us (0.45)
  waiting for transfers between devices: 787 us -> 0 us
  Pallas kernels: 0 us -> 406 us
  matrix products: 98.5 us -> 0 us
  between operations: 13.8 us -> 0.64 us
    unnamed x5 -> x0, waiting for transfers between devices: 493 us -> none
    pallas_call x0 -> x2, Pallas kernels: none -> 406 us  [the longest x1 400 us: local(): pl.pallas_call(functools.partial(_main, nr, nc), name='linear_backward',...]
    all_gather x2 -> x0, waiting for transfers between devices: 242 us -> none  [the longest x1 232 us: local(): w_col = lax.all_gather(w, 'r', axis=0, tiled=True)]
    dot_general x2 -> x0, matrix products: 98.5 us -> none  [the longest x1 49.9 us: local(): lax.dot_general(x_row, dy, (((0,), (0,)), ((), ())), preferred_element_ty...]
    reduce_scatter x1 -> x0, waiting for transfers between devices: 52.2 us -> none  [local(): lax.psum_scatter(dx_part, 'c', scatter_dimension=1, tiled=True)]
  transfers between devices with their start and end apart: 4 -> 0, of which waited for: 4 -> 0; matrix products, arithmetic and copies ran while one was open for 11% -> 0% of each run, Pallas kernels for 0% -> 0%
where the time goes in v2:
time: 408 us; the launch traced here: 406 us
  Pallas kernels  406 us (100%)
    pallas_call x1, Pallas kernels, local(): pl.pallas_call(functools.partial(_main, nr, nc), name='linear_backward',...  400 us

profile of v2, /device:TPU:101, one launch (start us, length us, event | category | flops | bytes accessed | tf_op | source)
XLA Modules:
  0.0 406.4 jit_solution(18022884808902140502)
XLA Ops:
  0.6 400.5 %linear_backward.1 = (f32[448,7168]{1,0:T(8,128)S(1)}, bf16[896,768]{1,0:T(8,128)(2,1)S(1)}, bf16[896,256]{1,0:T(8,128)(2,1)S(1)}, bf16[8,768,7168]{2,1,0:T(8,128)(2,1)}) custom-call(bf16[768,896]{1,0:T(8,128)(2,1)} %x.1, bf16[448,7168]{1,0:T(8,128)(2,1)} %w.1, bf16[768,7168]{1,0:T(8,128)(2,1)} %dy.1), custom_call_target="tpu_custom_call" | custom-call | tf_op jit(solution)/shard_map/linear_backward/pallas_call | solution.py:495
  401.1 5.3 %store.1 = (bf16[768,896]{1,0:T(8,128)(2,1)}, f32[448,7168]{1,0:T(8,128)}) custom-call(f32[448,7168]{1,0:T(8,128)S(1)} %get-tuple-element.5.dwv, bf16[896,768]{1,0:T(8,128)(2,1)S(1)} %get-tuple-element.6.dxb, bf16[896,256]{1,0:T(8,128)(2,1)S(1)} %get-tuple-element.7.dxl), custom_call_target="tpu_custom_call" | custom-call | tf_op jit(solution)/shard_map/store/pallas_call | solution.py:515

commit v3 on v2

--- a/solution.py
+++ b/solution.py
@@ -10,6 +10,8 @@
 MESH = pl.DeviceIdType.MESH
 ROWS = 128
 FIRST = 3
+MORE = 13
+THEN = 15
 SUB = 64
 TILE = 1024
 VMEM = 67043328
@@ -259,7 +261,8 @@
 
     def deliver_early(s):
         blka, ca, _, _ = where(s)
-        send_dx(s, pl.ds(0, m), blka, ca * ROWS, m)
+        for h in range(2):
+            send_dx(s, pl.ds(h * ROWS, ROWS), blka, (ca + h) * ROWS, ROWS)
 
     def deliver_late(s):
         blka, ca, blkb, cb = where(s)
@@ -339,11 +342,11 @@
         def _():
             deliver_early(s - 2)
 
-        per = -(-(early - FIRST) // runs)
+        per = -(-(MORE - FIRST) // runs)
         for d in range(per):
             old = FIRST + (s - early) * per + d
 
-            @pl.when((s >= early) & (old < early))
+            @pl.when((s >= early) & (old < MORE))
             def _():
                 deliver_early(old)
 
@@ -389,10 +392,14 @@
             dw_tiles(dyl, opp, runs, sibopp, runs, 0, 1)
         exchange_last(u)
         if u == 0:
+            for old in range(MORE, THEN):
+                deliver_early(jnp.int32(old))
             with jax.named_scope("reduce"):
                 sum_step(steps - 1)
 
     deliver_late(steps - 1)
+    for old in range(THEN, early):
+        deliver_early(jnp.int32(old))
     with jax.named_scope("dw"):
         dw_tiles(dyl, opp, runs, sibopp, runs, 1, nb // TILE)
     for u in range(subs - 1):

time: 408 us -> 407 us (level)
  no operation moved by 1% of the time
where the time goes in v3:
time: 407 us
  Pallas kernels  406 us (100%)
    pallas_call x1, Pallas kernels, local(): pl.pallas_call(functools.partial(_main, nr, nc), name='linear_backward',...  401 us

profile of v3, /device:TPU:101, one launch (start us, length us, event | category | flops | bytes accessed | tf_op | source)
XLA Modules:
  0.0 406.6 jit_solution(10002033009682700185)
XLA Ops:
  0.6 400.7 %linear_backward.1 = (f32[448,7168]{1,0:T(8,128)S(1)}, bf16[896,768]{1,0:T(8,128)(2,1)S(1)}, bf16[896,256]{1,0:T(8,128)(2,1)S(1)}, bf16[8,768,7168]{2,1,0:T(8,128)(2,1)}) custom-call(bf16[768,896]{1,0:T(8,128)(2,1)} %x.1, bf16[448,7168]{1,0:T(8,128)(2,1)} %w.1, bf16[768,7168]{1,0:T(8,128)(2,1)} %dy.1), custom_call_target="tpu_custom_call" | custom-call | tf_op jit(solution)/shard_map/linear_backward/pallas_call | solution.py:502
  401.4 5.3 %store.1 = (bf16[768,896]{1,0:T(8,128)(2,1)}, f32[448,7168]{1,0:T(8,128)}) custom-call(f32[448,7168]{1,0:T(8,128)S(1)} %get-tuple-element.5.dwv, bf16[896,768]{1,0:T(8,128)(2,1)S(1)} %get-tuple-element.6.dxb, bf16[896,256]{1,0:T(8,128)(2,1)S(1)} %get-tuple-element.7.dxl), custom_call_target="tpu_custom_call" | custom-call | tf_op jit(solution)/shard_map/store/pallas_call | solution.py:522

commit v4 on v3

--- a/solution.py
+++ b/solution.py
@@ -342,6 +342,10 @@
         def _():
             deliver_early(s - 2)
 
+        @pl.when(s > early)
+        def _():
+            deliver_late(s - 1)
+
         per = -(-(MORE - FIRST) // runs)
         for d in range(per):
             old = FIRST + (s - early) * per + d
@@ -349,10 +353,6 @@
             @pl.when((s >= early) & (old < MORE))
             def _():
                 deliver_early(old)
-
-        @pl.when(s > early)
-        def _():
-            deliver_late(s - 1)
 
         @pl.when(s < early - 1)
         def _():

time: 407 us -> 407 us (level)
  no operation moved by 1% of the time
where the time goes in v4:
time: 407 us
  Pallas kernels  406 us (100%)
    pallas_call x1, Pallas kernels, local(): pl.pallas_call(functools.partial(_main, nr, nc), name='linear_backward',...  401 us

profile of v4, /device:TPU:101, one launch (start us, length us, event | category | flops | bytes accessed | tf_op | source)
XLA Modules:
  0.0 407.0 jit_solution(16490501622664984680)
XLA Ops:
  0.6 401.1 %linear_backward.1 = (f32[448,7168]{1,0:T(8,128)S(1)}, bf16[896,768]{1,0:T(8,128)(2,1)S(1)}, bf16[896,256]{1,0:T(8,128)(2,1)S(1)}, bf16[8,768,7168]{2,1,0:T(8,128)(2,1)}) custom-call(bf16[768,896]{1,0:T(8,128)(2,1)} %x.1, bf16[448,7168]{1,0:T(8,128)(2,1)} %w.1, bf16[768,7168]{1,0:T(8,128)(2,1)} %dy.1), custom_call_target="tpu_custom_call" | custom-call | tf_op jit(solution)/shard_map/linear_backward/pallas_call | solution.py:502
  401.7 5.3 %store.1 = (bf16[768,896]{1,0:T(8,128)(2,1)}, f32[448,7168]{1,0:T(8,128)}) custom-call(f32[448,7168]{1,0:T(8,128)S(1)} %get-tuple-element.5.dwv, bf16[896,768]{1,0:T(8,128)(2,1)S(1)} %get-tuple-element.6.dxb, bf16[896,256]{1,0:T(8,128)(2,1)S(1)} %get-tuple-element.7.dxl), custom_call_target="tpu_custom_call" | custom-call | tf_op jit(solution)/shard_map/store/pallas_call | solution.py:522
